TPU v7x, 32 devices: a whole 2x2x4 slice. The times are simulated.
32 devices in a mesh: slab: 8 (over y, x, core), chan: 4 (over z).
Axes of the slice: x: 2, y: 2, z: 4, core: 2. Of those that a mesh axis runs over, the one named last changes fastest.
Arguments:
- features: bfloat16 [96, 16384], P('chan', 'slab'), may hold values from -1 to 3
- coords: bfloat16 [3, 16384], P(None, 'slab'), may hold values from 0 to 1
- send_rows: int32 [2, 8192], P(None, 'slab'), may hold values from 0 to 2047
- send_count: int32 [2, 8], P(None, 'slab'), may hold values from 1 to 1024, as said below
- neighbours: int32 [1024, 128], P('slab'), may hold values from 0 to 4095, as said below
- neighbour_count: int32 [1024], P('slab'), may hold values from 32 to 128
- geom_weight: bfloat16 [80, 6], replicated, may hold values from -3.5 to 3.5
- feat_weight: bfloat16 [80, 96], replicated, may hold values from -0.625 to 0.625
- bias_one: float32 [80], replicated, may hold values from -3 to 3
- hidden_weight: bfloat16 [80, 80], replicated, may hold values from -1 to 1
- bias_two: float32 [80], replicated, may hold values from -3 to 3
- out_weight: bfloat16 [96, 80], replicated, may hold values from -1 to 1
- bias_three: float32 [96], replicated, may hold values from -3 to 3
Outputs:
- latent: float32 [96, 1024], P('chan', 'slab')
Inputs may be any that keep to these rules, and one draw needn't show every extreme that they name: `send_count`: every slab has at least one live slot in each direction; some slab has all 1024 slots of its lower list live. `neighbours`: entries index the slab's point table: below 2048 own points, then 1024 slots from the slab below, then 1024 from the slab above; slot 0 of every node is an own point; nodes of the lower plane of a slab use the slots from below, those of the upper plane the slots from above, and may name dead slots.
All inputs are finite; a program needn't handle non-finite values.
Results may differ from a plain program's by a relative error of at most 0.0013.
Values may be sent and summed in bfloat16 or wider, within the bound.
No kernel may reach another device: no remote copies, remote signals or barrier semaphores. Data moves between devices by JAX's collectives and lax.ppermute only.
A program may use at most 64 MiB of HBM per device.

v0:
```python
import jax
import jax.numpy as jnp
from jax import lax
from jax.sharding import PartitionSpec as P

ZD = 2
GX = 16
GY = 4


def padded(block, sides, width):
    for axis, dim in sides:
        count = lax.axis_size(axis)
        forward = [(i, i + 1) for i in range(count - 1)]
        backward = [(target, source) for source, target in forward]
        low = lax.ppermute(
            lax.slice_in_dim(block, block.shape[dim] - width, None, axis=dim), axis, forward
        )
        high = lax.ppermute(lax.slice_in_dim(block, 0, width, axis=dim), axis, backward)
        block = jnp.concatenate([low, block, high], axis=dim)
    return block


def node_term(geom_weight, bias_one, node_ids, depth):
    along_x = ((node_ids % GX).astype(jnp.float32) + 0.5) / GX
    along_y = ((node_ids // GX % GY).astype(jnp.float32) + 0.5) / GY
    along_z = ((node_ids // (GX * GY)).astype(jnp.float32) + 0.5) / depth
    geom = geom_weight[:, 0:3].astype(jnp.float32)
    return (
        geom[:, 0:1] * along_x[None, :]
        + geom[:, 1:2] * along_y[None, :]
        + geom[:, 2:3] * along_z[None, :]
        + bias_one[:, None]
    )


def kernel_block(
    pre_table,
    value_table,
    flag_table,
    nbr,
    counts,
    node_pre,
    hidden_weight,
    bias_two,
    out_rows,
    bias_rows,
):
    nodes, slots = nbr.shape
    hidden = pre_table.shape[0]
    flat = nbr.reshape(-1)
    gathered = jnp.take(pre_table, flat, axis=1).astype(jnp.float32).reshape(hidden, nodes, slots)
    first = (
        jax.nn.gelu(gathered + node_pre[:, :, None])
        .reshape(hidden, nodes * slots)
        .astype(jnp.bfloat16)
    )
    second = jax.nn.gelu(
        jnp.dot(hidden_weight, first, preferred_element_type=jnp.float32) + bias_two[:, None]
    ).astype(jnp.bfloat16)
    kappa = jnp.dot(out_rows, second, preferred_element_type=jnp.float32) + bias_rows[:, None]
    values = jnp.take(value_table, flat, axis=1).astype(jnp.float32)
    used = (jnp.arange(slots, dtype=jnp.int32)[None, :] < counts[:, None]).astype(jnp.float32)
    flags = jnp.take(flag_table, flat).astype(jnp.float32) * used.reshape(-1)
    total = (kappa * values * flags[None, :]).reshape(out_rows.shape[0], nodes, slots).sum(axis=2)
    weight = flags.reshape(nodes, slots).sum(axis=1)
    return total / weight[None, :]


def encode(
    pre_table,
    value_table,
    flag_table,
    nbr,
    counts,
    first_id,
    depth,
    geom_weight,
    bias_one,
    hidden_weight,
    bias_two,
    out_rows,
    bias_rows,
):
    nodes = nbr.shape[0]
    block = min(128, nodes)
    blocks = nodes // block

    def one_block(index):
        start = index * block
        ids = first_id + start + jnp.arange(block, dtype=jnp.int32)
        node_pre = node_term(geom_weight, bias_one, ids, depth)
        return kernel_block(
            pre_table,
            value_table,
            flag_table,
            nbr,
            counts,
            node_pre,
            hidden_weight,
            bias_two,
            out_rows,
            bias_rows,
        )

    result = lax.map(one_block, jnp.arange(blocks, dtype=jnp.int32))
    return result.transpose(1, 0, 2).reshape(out_rows.shape[0], nodes)


def shards(
    features,
    coords,
    send_rows,
    send_count,
    neighbours,
    neighbour_count,
    geom_weight,
    feat_weight,
    bias_one,
    hidden_weight,
    bias_two,
    out_weight,
    bias_three,
):
    groups = lax.axis_size("chan")
    member = lax.axis_index("chan")
    slab_id = lax.axis_index("slab")
    depth = ZD * lax.axis_size("slab")
    own_full = lax.all_gather(features, "chan", axis=0, tiled=True)
    pre_own = (
        jnp.dot(feat_weight, own_full, preferred_element_type=jnp.float32)
        + jnp.dot(geom_weight[:, 3:6], coords, preferred_element_type=jnp.float32)
    ).astype(jnp.bfloat16)
    send = send_rows.shape[1]
    points = features.shape[1]
    hidden = pre_own.shape[0]
    chans = own_full.shape[0]
    columns = send_rows.reshape(-1)
    live = (
        (jnp.arange(send, dtype=jnp.int32)[None, :] < send_count)
        .astype(jnp.bfloat16)
        .reshape(1, 2 * send)
    )
    pre_sel = jnp.take(pre_own, columns, axis=1)
    val_sel = jnp.take(own_full, columns, axis=1)
    ones_row = jnp.ones((1, 2 * send), jnp.bfloat16)
    payload = jnp.concatenate([pre_sel, val_sel, ones_row], axis=0) * live
    extended = padded(payload, (("slab", 1),), send)
    below = extended[:, :send]
    above = extended[:, 3 * send :]
    below_pre = below[:hidden]
    above_pre = above[:hidden]
    below_vals = below[hidden : hidden + chans]
    above_vals = above[hidden : hidden + chans]
    below_flag = below[hidden + chans]
    above_flag = above[hidden + chans]
    pre_table = jnp.concatenate([pre_own, below_pre, above_pre], axis=1)
    value_table = jnp.concatenate([own_full, below_vals, above_vals], axis=1)
    flag_table = jnp.concatenate(
        [jnp.ones((points,), jnp.bfloat16), below_flag, above_flag], axis=0
    )
    per_slab = neighbours.shape[0]
    share = per_slab // groups
    start = member * share
    part_nbr = lax.dynamic_slice_in_dim(neighbours, start, share, 0)
    part_cnt = lax.dynamic_slice_in_dim(neighbour_count, start, share, 0)
    partial_value = encode(
        pre_table,
        value_table,
        flag_table,
        part_nbr,
        part_cnt,
        slab_id * per_slab + start,
        depth,
        geom_weight,
        bias_one,
        hidden_weight,
        bias_two,
        out_weight,
        bias_three,
    )
    return lax.all_to_all(partial_value, "chan", split_axis=0, concat_axis=1, tiled=True)


def solution(mesh):
    placed = (
        P("chan", "slab"),
        P(None, "slab"),
        P(None, "slab"),
        P(None, "slab"),
        P("slab", None),
        P("slab"),
        P(),
        P(),
        P(),
        P(),
        P(),
        P(),
        P(),
    )
    return jax.shard_map(
        shards, mesh=mesh, in_specs=placed, out_specs=P("chan", "slab"), check_vma=False
    )
```

profile of v0, /device:TPU:1, one launch (start us, length us, event | category | flops | bytes accessed | tf_op | source)
XLA Modules:
  0.0 116.7 jit_solution(4114827480123415698)
XLA Ops:
  0.0 0.7 compare_and_fusion.1
  0.8 0.7 fusion.37
  1.5 0.7 copy.71
  2.2 14.1 %all_gather.3 = bf16[96,2048]{1,0:T(8,128)(2,1)S(1)} all-gather(bf16[24,2048]{1,0:T(8,128)(2,1)} %param.13), channel_id=1, replica_groups=mesh['slab'=8,'chan'=4] {'chan'}, dimensions={0}, use_global_device_ids=true | all-gather | bytes 491520 | tf_op jit(solution)/shard_map/all_gather | solution.py:129
  16.9 0.3 fusion.3
  17.4 6.2 %gather_fusion = bf16[2048,80]{1,0:T(8,128)(2,1)S(1)} fusion(bf16[80,2048]{0,1:T(8,128)(2,1)S(1)} %copy.55, s32[2048]{0:T(1024)S(1)} %broadcast_clamp_fusion.1), kind=kCustom, calls=%fused_computation | custom fusion | bytes 663552 | tf_op jit(solution)/shard_map/jit(_take)/gather | solution.py:144
  23.9 6.2 %gather_fusion.1 = bf16[2048,96]{1,0:T(8,128)(2,1)S(1)} fusion(bf16[96,2048]{0,1:T(8,128)(2,1)S(1)} %copy.57, s32[2048]{0:T(1024)S(1)} %broadcast_clamp_fusion.1), kind=kCustom, calls=%fused_computation.1 | custom fusion | bytes 794624 | tf_op jit(solution)/shard_map/jit(_take)/gather | solution.py:145
  30.7 5.4 %collective-permute-start = (bf16[177,1024]{1,0:T(8,128)(2,1)S(1)}, bf16[177,1024]{1,0:T(8,128)(2,1)S(1)}, u32[]{:S(2)}, u32[]{:S(2)}) collective-permute-start(bf16[177,1024]{1,0:T(8,128)(2,1)S(1)} %get-tuple-element.33), channel_id=1, source_target_pairs={{0,4},{4,8},{8,12},{12,16},{16,20},{20,24},{24,28},{1,5},{5,9},{9,... | collective-permute-start | bytes 1087496 | tf_op jit(solution)/shard_map/ppermute | solution.py:16
  36.2 1.9 %collective-permute-start.1 = (bf16[177,1024]{1,0:T(8,128)(2,1)S(1)}, bf16[177,1024]{1,0:T(8,128)(2,1)S(1)}, u32[]{:S(2)}, u32[]{:S(2)}) collective-permute-start(bf16[177,1024]{1,0:T(8,128)(2,1)S(1)} %get-tuple-element.34), channel_id=1, source_target_pairs={{4,0},{8,4},{12,8},{16,12},{20,16},{24,20},{28,24},{5,1},{9,5},{13... | collective-permute-start | bytes 1087496 | tf_op jit(solution)/shard_map/ppermute | solution.py:19
  38.5 2.2 %collective-permute-done = bf16[177,1024]{1,0:T(8,128)(2,1)S(1)} collective-permute-done((bf16[177,1024]{1,0:T(8,128)(2,1)S(1)}, bf16[177,1024]{1,0:T(8,128)(2,1)S(1)}, u32[]{:S(2)}, u32[]{:S(2)}) %collective-permute-start) | collective-permute-done | bytes 362528 | tf_op jit(solution)/shard_map/ppermute | solution.py:16
  40.7 5.7 %collective-permute-done.1 = bf16[177,1024]{1,0:T(8,128)(2,1)S(1)} collective-permute-done((bf16[177,1024]{1,0:T(8,128)(2,1)S(1)}, bf16[177,1024]{1,0:T(8,128)(2,1)S(1)}, u32[]{:S(2)}, u32[]{:S(2)}) %collective-permute-start.1) | collective-permute-done | bytes 362528 | tf_op jit(solution)/shard_map/ppermute | solution.py:19
  46.4 25.6 %gather_fusion.4 = bf16[4096]{0:T(1024)(128)(2,1)S(1)} fusion(bf16[4096]{0:T(1024)(128)(2,1)S(1)} %pad_maximum_fusion.2, s32[4096]{0:T(1024)S(1)} %broadcast_clamp_fusion), kind=kCustom, calls=%fused_computation.4 | custom fusion | bytes 32768 | tf_op jit(solution)/shard_map/while/body/eval_jaxpr/jit(_take)/gather | solution.py:64
  73.0 12.1 %gather_fusion.3 = bf16[4096,96]{1,0:T(8,128)(2,1)S(1)} fusion(bf16[96,4096]{0,1:T(8,128)(2,1)S(1)} %pad_maximum_fusion, s32[4096]{0:T(1024)S(1)} %broadcast_clamp_fusion), kind=kCustom, calls=%fused_computation.3 | custom fusion | bytes 1589248 | tf_op jit(solution)/shard_map/while/body/eval_jaxpr/jit(_take)/gather | solution.py:62
  85.1 1.2 %copy.65 = bf16[4096,96]{0,1:T(8,128)(2,1)} copy(bf16[4096,96]{1,0:T(8,128)(2,1)S(1)} %gather_fusion.3) | data formatting | bytes 1572864 | tf_op jit(solution)/shard_map/while/body/eval_jaxpr/jit(_take)/gather | solution.py:62
  86.4 0.6 copy.59
  87.1 12.1 %gather_fusion.2 = bf16[4096,80]{1,0:T(8,128)(2,1)S(1)} fusion(bf16[80,4096]{0,1:T(8,128)(2,1)S(1)} %copy.59, s32[4096]{0:T(1024)S(1)} %broadcast_clamp_fusion), kind=kCustom, calls=%fused_computation.2 | custom fusion | bytes 1327104 | tf_op jit(solution)/shard_map/while/body/eval_jaxpr/jit(_take)/gather | solution.py:52
  99.2 1.3 %copy.60 = bf16[4096,80]{0,1:T(8,128)(2,1)} copy(bf16[4096,80]{1,0:T(8,128)(2,1)S(1)} %gather_fusion.2) | data formatting | bytes 1310720 | tf_op jit(solution)/shard_map/while/body/eval_jaxpr/jit(_take)/gather | solution.py:52
  100.5 0.4 add.268
  100.9 3.2 %fusion.4 = f32[12,8,32,128]{3,1,2,0:T(8,128)S(1)} fusion(bf16[96,80]{0,1:T(8,128)(2,1)S(1)} %copy-done, bf16[80,80]{1,0:T(8,128)(2,1)S(1)} %copy-done.8, f32[4096]{0:T(1024)S(1)} %get-tuple-element.31, bf16[4096,96]{0,1:T(8,128)(2,1)} %copy.65, f32[96]{0:T(128)S(1)} %copy-done.10, pred[4096]{0:T(1024)(128)(4,1)S(1)} %get-tuple-element.32, ...), kind=kOutput, calls=%fused_computation.14 | convolution fusion | flops 124518400 | bytes 4374720 | tf_op jit(solution)/shard_map/while/body/eval_jaxpr/dot_general | solution.py:61
  104.5 0.5 reduce_sum.22
  105.3 9.4 %all_to_all.16 = f32[4,1,768]{2,1,0:T(1,128)S(1)} all-to-all(f32[4,1,768]{2,1,0:T(1,128)S(1)} %reshape.384), channel_id=1, replica_groups=mesh['slab'=8,'chan'=4] {'chan'}, dimensions={0} | all-to-all | bytes 24576 | tf_op jit(solution)/shard_map/all_to_all | solution.py:182
  114.7 0.5 broadcast.479
  115.2 0.7 reduce.4
  116.0 0.7 all_to_all.14
  (70 shorter events, 3.7 us)
Async XLA Ops:
  0.0 100.9 %copy-start = (bf16[96,80]{0,1:T(8,128)(2,1)S(1)}, bf16[96,80]{0,1:T(8,128)(2,1)}, u32[]{:S(2)}) copy-start(bf16[96,80]{0,1:T(8,128)(2,1)} %param.24) | copy-start | bytes 46084
  0.0 16.6 %copy-start.4 = (bf16[80,96]{1,0:T(8,128)(2,1)S(1)}, bf16[80,96]{1,0:T(8,128)(2,1)}, u32[]{:S(2)}) copy-start(bf16[80,96]{1,0:T(8,128)(2,1)} %param.20) | copy-start | bytes 46084
  0.0 16.8 %copy-start.6 = (bf16[80,6]{0,1:T(8,128)(2,1)S(1)}, bf16[80,6]{0,1:T(8,128)(2,1)}, u32[]{:S(2)}) copy-start(bf16[80,6]{0,1:T(8,128)(2,1)} %param.19) | copy-start | bytes 2884
  0.0 16.8 %copy-start.5 = (bf16[3,2048]{1,0:T(4,128)(2,1)S(1)}, bf16[3,2048]{1,0:T(4,128)(2,1)}, u32[]{:S(2)}) copy-start(bf16[3,2048]{1,0:T(4,128)(2,1)} %param.14) | copy-start | bytes 36868
  30.4 7.7 %copy-start.3 = (s32[128,128]{1,0:T(8,128)S(1)}, s32[128,128]{1,0:T(8,128)}, u32[]{:S(2)}) copy-start(s32[128,128]{1,0:T(8,128)} %param.17) | copy-start | bytes 196612
  30.4 7.8 %copy-start.7 = (f32[80]{0:T(128)S(1)}, f32[80]{0:T(128)}, u32[]{:S(2)}) copy-start(f32[80]{0:T(128)} %param.21) | copy-start | bytes 964
  30.4 7.9 %copy-start.9 = (s32[128]{0:T(128)S(1)}, s32[128]{0:T(128)}, u32[]{:S(2)}) copy-start(s32[128]{0:T(128)} %param.18) | copy-start | bytes 1540
  30.7 10.0 %collective-permute-start = (bf16[177,1024]{1,0:T(8,128)(2,1)S(1)}, bf16[177,1024]{1,0:T(8,128)(2,1)S(1)}, u32[]{:S(2)}, u32[]{:S(2)}) collective-permute-start(bf16[177,1024]{1,0:T(8,128)(2,1)S(1)} %get-tuple-element.33), channel_id=1, source_target_pairs={{0,4},{4,8},{8,12},{12,16},{16,20},{20,24},{24,28},{1,5},{5,9},{9,... | collective-permute-start | bytes 1087496 | tf_op jit(solution)/shard_map/ppermute | solution.py:16
  36.2 10.2 %collective-permute-start.1 = (bf16[177,1024]{1,0:T(8,128)(2,1)S(1)}, bf16[177,1024]{1,0:T(8,128)(2,1)S(1)}, u32[]{:S(2)}, u32[]{:S(2)}) collective-permute-start(bf16[177,1024]{1,0:T(8,128)(2,1)S(1)} %get-tuple-element.34), channel_id=1, source_target_pairs={{4,0},{8,4},{12,8},{16,12},{20,16},{24,20},{28,24},{5,1},{9,5},{13... | collective-permute-start | bytes 1087496 | tf_op jit(solution)/shard_map/ppermute | solution.py:19
  40.7 31.6 %copy-start.1 = (bf16[177,1024]{1,0:T(8,128)(2,1)}, bf16[177,1024]{1,0:T(8,128)(2,1)S(1)}, u32[]{:S(2)}) copy-start(bf16[177,1024]{1,0:T(8,128)(2,1)S(1)} %collective-permute-done) | copy-start | bytes 1087492
  46.4 26.1 %copy-start.2 = (bf16[177,1024]{1,0:T(8,128)(2,1)}, bf16[177,1024]{1,0:T(8,128)(2,1)S(1)}, u32[]{:S(2)}) copy-start(bf16[177,1024]{1,0:T(8,128)(2,1)S(1)} %collective-permute-done.1) | copy-start | bytes 1087492
  85.1 1.3 %slice-start = ((bf16[177,1024]{1,0:T(8,128)(2,1)}), bf16[80,1024]{1,0:T(8,128)(2,1)S(1)}, s32[]{:S(2)}) async-start(bf16[177,1024]{1,0:T(8,128)(2,1)} %copy-done.1), calls=%async_computation.1 | async-start | bytes 327680 | tf_op jit(solution)/shard_map/slice | solution.py:151
  85.1 1.3 %slice-start.1 = ((bf16[177,1024]{1,0:T(8,128)(2,1)}), bf16[80,1024]{1,0:T(8,128)(2,1)S(1)}, s32[]{:S(2)}) async-start(bf16[177,1024]{1,0:T(8,128)(2,1)} %copy-done.2), calls=%async_computation.2 | async-start | bytes 327680 | tf_op jit(solution)/shard_map/slice | solution.py:152
  99.2 1.7 %copy-start.8 = (bf16[80,80]{1,0:T(8,128)(2,1)S(1)}, bf16[80,80]{1,0:T(8,128)(2,1)}, u32[]{:S(2)}) copy-start(bf16[80,80]{1,0:T(8,128)(2,1)} %param.22) | copy-start | bytes 38404
  99.2 1.7 %copy-start.10 = (f32[96]{0:T(128)S(1)}, f32[96]{0:T(128)}, u32[]{:S(2)}) copy-start(f32[96]{0:T(128)} %param.25) | copy-start | bytes 1156
  99.2 1.7 %copy-start.11 = (f32[80]{0:T(128)S(1)}, f32[80]{0:T(128)}, u32[]{:S(2)}) copy-start(f32[80]{0:T(128)} %param.23) | copy-start | bytes 964
where the time goes:
time: 117 us
  local copies, waits for them, and re-layouts  70.1 us (60%)
  blocking collectives  23.4 us (20%)
  waiting for transfers between devices  7.85 us (7%)
  starting transfers between devices  7.34 us (6%)
  matrix products  3.76 us (3%)
  other arithmetic  3.72 us (3%)
    gather x1, local copies, waits for them, and re-layouts, kernel_block(): flags = jnp.take(flag_table, flat).astype(jnp.float32) * used.reshape(-1)  25.6 us
    all_gather x1, blocking collectives, shards(): own_full = lax.all_gather(features, 'chan', axis=0, tiled=True)  14.1 us
    gather x2, local copies, waits for them, and re-layouts, kernel_block(): jnp.take(pre_table, flat, axis=1).astype(jnp.float32)  13.4 us
    gather x2, local copies, waits for them, and re-layouts, kernel_block(): values = jnp.take(value_table, flat, axis=1).astype(jnp.float32)  13.4 us
    all_to_all x1, blocking collectives, shards(): lax.all_to_all(partial_value, 'chan', split_axis=0, concat_axis=1, tiled=...  9.35 us
    gather x2, local copies, waits for them, and re-layouts, shards(): val_sel = jnp.take(own_full, columns, axis=1)  6.4 us
    gather x2, local copies, waits for them, and re-layouts, shards(): pre_sel = jnp.take(pre_own, columns, axis=1)  6.4 us
    ppermute x1, waiting for transfers between devices, padded(): lax.ppermute(lax.slice_in_dim(block, 0, width, axis=dim), axis, backward)  5.67 us
  transfers between devices with their start and end apart: 2, of which 2 were waited for; matrix products, arithmetic and copies ran while one was open for 0% of the time, Pallas kernels for 0%

commit v1 on v0

--- a/solution.py
+++ b/solution.py
@@ -1,11 +1,25 @@
+import functools
 import jax
 import jax.numpy as jnp
 from jax import lax
 from jax.sharding import PartitionSpec as P
+from jax.lax import all_to_all, axis_size
 
 ZD = 2
 GX = 16
 GY = 4
+
+
+def pack_rails(buf, lane_axis, pos_dim, out_dim):
+    return jnp.concatenate(
+        all_to_all(
+            jnp.stack(jnp.split(buf, axis_size(lane_axis), axis=pos_dim), 0), lane_axis, 0, 0
+        ),
+        axis=out_dim,
+    )
+
+
+point_packet = functools.partial(pack_rails, lane_axis="chan", pos_dim=0, out_dim=1)
 
 
 def padded(block, sides, width):
@@ -179,7 +193,7 @@
         out_weight,
         bias_three,
     )
-    return lax.all_to_all(partial_value, "chan", split_axis=0, concat_axis=1, tiled=True)
+    return point_packet(partial_value)
 
 
 def solution(mesh):

time: 117 us -> 117 us (level)
  no operation moved by 1% of the time
where the time goes in v1:
time: 117 us; the launch traced here: 116 us
  local copies, waits for them, and re-layouts  70 us (60%)
  blocking collectives  23.4 us (20%)
  waiting for transfers between devices  7.85 us (7%)
  starting transfers between devices  7.34 us (6%)
  matrix products  3.76 us (3%)
  other arithmetic  3.63 us (3%)
    gather x1, local copies, waits for them, and re-layouts, kernel_block(): flags = jnp.take(flag_table, flat).astype(jnp.float32) * used.reshape(-1)  25.6 us
    all_gather x1, blocking collectives, shards(): own_full = lax.all_gather(features, 'chan', axis=0, tiled=True)  14.1 us
    gather x2, local copies, waits for them, and re-layouts, kernel_block(): values = jnp.take(value_table, flat, axis=1).astype(jnp.float32)  13.4 us
    gather x2, local copies, waits for them, and re-layouts, kernel_block(): jnp.take(pre_table, flat, axis=1).astype(jnp.float32)  13.4 us
    all_to_all x1, blocking collectives, pack_rails(): all_to_all(jnp.stack(jnp.split(buf, axis_size(lane_axis), axis=pos_dim),...  9.35 us
    gather x2, local copies, waits for them, and re-layouts, shards(): val_sel = jnp.take(own_full, columns, axis=1)  6.4 us
    gather x2, local copies, waits for them, and re-layouts, shards(): pre_sel = jnp.take(pre_own, columns, axis=1)  6.4 us
    ppermute x1, waiting for transfers between devices, padded(): lax.ppermute(lax.slice_in_dim(block, 0, width, axis=dim), axis, backward)  5.67 us
  transfers between devices with their start and end apart: 2, of which 2 were waited for; matrix products, arithmetic and copies ran while one was open for 0% of the time, Pallas kernels for 0%

profile of v1, /device:TPU:1, one launch (start us, length us, event | category | flops | bytes accessed | tf_op | source)
XLA Modules:
  0.0 116.5 jit_solution(12410105156077738369)
XLA Ops:
  0.0 0.7 compare_and_fusion.1
  0.8 0.7 fusion.37
  1.5 0.7 copy.72
  2.2 14.1 %all_gather.3 = bf16[96,2048]{1,0:T(8,128)(2,1)S(1)} all-gather(bf16[24,2048]{1,0:T(8,128)(2,1)} %param.13), channel_id=1, replica_groups=mesh['slab'=8,'chan'=4] {'chan'}, dimensions={0}, use_global_device_ids=true | all-gather | bytes 491520 | tf_op jit(solution)/shard_map/all_gather | solution.py:143
  16.9 0.3 fusion.3
  17.4 6.2 %gather_fusion = bf16[2048,80]{1,0:T(8,128)(2,1)S(1)} fusion(bf16[80,2048]{0,1:T(8,128)(2,1)S(1)} %copy.59, s32[2048]{0:T(1024)S(1)} %broadcast_clamp_fusion.1), kind=kCustom, calls=%fused_computation | custom fusion | bytes 663552 | tf_op jit(solution)/shard_map/jit(_take)/gather | solution.py:158
  23.9 6.2 %gather_fusion.1 = bf16[2048,96]{1,0:T(8,128)(2,1)S(1)} fusion(bf16[96,2048]{0,1:T(8,128)(2,1)S(1)} %copy.61, s32[2048]{0:T(1024)S(1)} %broadcast_clamp_fusion.1), kind=kCustom, calls=%fused_computation.1 | custom fusion | bytes 794624 | tf_op jit(solution)/shard_map/jit(_take)/gather | solution.py:159
  30.7 5.4 %collective-permute-start = (bf16[177,1024]{1,0:T(8,128)(2,1)S(1)}, bf16[177,1024]{1,0:T(8,128)(2,1)S(1)}, u32[]{:S(2)}, u32[]{:S(2)}) collective-permute-start(bf16[177,1024]{1,0:T(8,128)(2,1)S(1)} %get-tuple-element.33), channel_id=1, source_target_pairs={{0,4},{4,8},{8,12},{12,16},{16,20},{20,24},{24,28},{1,5},{5,9},{9,... | collective-permute-start | bytes 1087496 | tf_op jit(solution)/shard_map/ppermute | solution.py:30
  36.2 1.9 %collective-permute-start.1 = (bf16[177,1024]{1,0:T(8,128)(2,1)S(1)}, bf16[177,1024]{1,0:T(8,128)(2,1)S(1)}, u32[]{:S(2)}, u32[]{:S(2)}) collective-permute-start(bf16[177,1024]{1,0:T(8,128)(2,1)S(1)} %get-tuple-element.34), channel_id=1, source_target_pairs={{4,0},{8,4},{12,8},{16,12},{20,16},{24,20},{28,24},{5,1},{9,5},{13... | collective-permute-start | bytes 1087496 | tf_op jit(solution)/shard_map/ppermute | solution.py:33
  38.5 2.2 %collective-permute-done = bf16[177,1024]{1,0:T(8,128)(2,1)S(1)} collective-permute-done((bf16[177,1024]{1,0:T(8,128)(2,1)S(1)}, bf16[177,1024]{1,0:T(8,128)(2,1)S(1)}, u32[]{:S(2)}, u32[]{:S(2)}) %collective-permute-start) | collective-permute-done | bytes 362528 | tf_op jit(solution)/shard_map/ppermute | solution.py:30
  40.7 5.7 %collective-permute-done.1 = bf16[177,1024]{1,0:T(8,128)(2,1)S(1)} collective-permute-done((bf16[177,1024]{1,0:T(8,128)(2,1)S(1)}, bf16[177,1024]{1,0:T(8,128)(2,1)S(1)}, u32[]{:S(2)}, u32[]{:S(2)}) %collective-permute-start.1) | collective-permute-done | bytes 362528 | tf_op jit(solution)/shard_map/ppermute | solution.py:33
  46.4 25.6 %gather_fusion.4 = bf16[4096]{0:T(1024)(128)(2,1)S(1)} fusion(bf16[4096]{0:T(1024)(128)(2,1)S(1)} %pad_maximum_fusion.3, s32[4096]{0:T(1024)S(1)} %broadcast_clamp_fusion), kind=kCustom, calls=%fused_computation.4 | custom fusion | bytes 32768 | tf_op jit(solution)/shard_map/while/body/eval_jaxpr/jit(_take)/gather | solution.py:78
  73.0 12.1 %gather_fusion.3 = bf16[4096,96]{1,0:T(8,128)(2,1)S(1)} fusion(bf16[96,4096]{0,1:T(8,128)(2,1)S(1)} %pad_maximum_fusion, s32[4096]{0:T(1024)S(1)} %broadcast_clamp_fusion), kind=kCustom, calls=%fused_computation.3 | custom fusion | bytes 1589248 | tf_op jit(solution)/shard_map/while/body/eval_jaxpr/jit(_take)/gather | solution.py:76
  85.1 1.3 %copy.69 = bf16[4096,96]{0,1:T(8,128)(2,1)} copy(bf16[4096,96]{1,0:T(8,128)(2,1)S(1)} %gather_fusion.3) | data formatting | bytes 1572864 | tf_op jit(solution)/shard_map/while/body/eval_jaxpr/jit(_take)/gather | solution.py:76
  86.4 0.6 copy.63
  87.1 12.1 %gather_fusion.2 = bf16[4096,80]{1,0:T(8,128)(2,1)S(1)} fusion(bf16[80,4096]{0,1:T(8,128)(2,1)S(1)} %copy.63, s32[4096]{0:T(1024)S(1)} %broadcast_clamp_fusion), kind=kCustom, calls=%fused_computation.2 | custom fusion | bytes 1327104 | tf_op jit(solution)/shard_map/while/body/eval_jaxpr/jit(_take)/gather | solution.py:66
  99.3 1.3 %copy.64 = bf16[4096,80]{0,1:T(8,128)(2,1)} copy(bf16[4096,80]{1,0:T(8,128)(2,1)S(1)} %gather_fusion.2) | data formatting | bytes 1310720 | tf_op jit(solution)/shard_map/while/body/eval_jaxpr/jit(_take)/gather | solution.py:66
  100.5 0.4 add.268
  101.0 3.2 %fusion.4 = f32[12,8,32,128]{3,1,2,0:T(8,128)S(1)} fusion(bf16[96,80]{0,1:T(8,128)(2,1)S(1)} %copy-done, bf16[80,80]{1,0:T(8,128)(2,1)S(1)} %copy-done.8, f32[4096]{0:T(1024)S(1)} %get-tuple-element.31, bf16[4096,96]{0,1:T(8,128)(2,1)} %copy.69, f32[96]{0:T(128)S(1)} %copy-done.10, pred[4096]{0:T(1024)(128)(4,1)S(1)} %get-tuple-element.32, ...), kind=kOutput, calls=%fused_computation.14 | convolution fusion | flops 124518400 | bytes 4374720 | tf_op jit(solution)/shard_map/while/body/eval_jaxpr/dot_general | solution.py:75
  104.5 0.5 reduce_sum.20
  105.1 9.3 %all_to_all.5 = f32[4,1,768]{2,1,0:T(1,128)S(1)} all-to-all(f32[4,1,768]{2,1,0:T(1,128)S(1)} %reshape.383), channel_id=1, replica_groups=mesh['slab'=8,'chan'=4] {'chan'}, dimensions={0} | all-to-all | bytes 24576 | tf_op jit(solution)/shard_map/all_to_all | solution.py:15
  114.5 0.5 broadcast.477
  115.0 0.7 reduce.4
  115.8 0.7 reshape.338
  (70 shorter events, 3.5 us)
Async XLA Ops:
  0.0 101.0 %copy-start = (bf16[96,80]{0,1:T(8,128)(2,1)S(1)}, bf16[96,80]{0,1:T(8,128)(2,1)}, u32[]{:S(2)}) copy-start(bf16[96,80]{0,1:T(8,128)(2,1)} %param.24) | copy-start | bytes 46084
  0.0 16.6 %copy-start.4 = (bf16[80,96]{1,0:T(8,128)(2,1)S(1)}, bf16[80,96]{1,0:T(8,128)(2,1)}, u32[]{:S(2)}) copy-start(bf16[80,96]{1,0:T(8,128)(2,1)} %param.20) | copy-start | bytes 46084
  0.0 16.8 %copy-start.6 = (bf16[80,6]{0,1:T(8,128)(2,1)S(1)}, bf16[80,6]{0,1:T(8,128)(2,1)}, u32[]{:S(2)}) copy-start(bf16[80,6]{0,1:T(8,128)(2,1)} %param.19) | copy-start | bytes 2884
  0.0 16.8 %copy-start.5 = (bf16[3,2048]{1,0:T(4,128)(2,1)S(1)}, bf16[3,2048]{1,0:T(4,128)(2,1)}, u32[]{:S(2)}) copy-start(bf16[3,2048]{1,0:T(4,128)(2,1)} %param.14) | copy-start | bytes 36868
  30.4 7.7 %copy-start.3 = (s32[128,128]{1,0:T(8,128)S(1)}, s32[128,128]{1,0:T(8,128)}, u32[]{:S(2)}) copy-start(s32[128,128]{1,0:T(8,128)} %param.17) | copy-start | bytes 196612
  30.4 7.8 %copy-start.7 = (f32[80]{0:T(128)S(1)}, f32[80]{0:T(128)}, u32[]{:S(2)}) copy-start(f32[80]{0:T(128)} %param.21) | copy-start | bytes 964
  30.4 7.9 %copy-start.9 = (s32[128]{0:T(128)S(1)}, s32[128]{0:T(128)}, u32[]{:S(2)}) copy-start(s32[128]{0:T(128)} %param.18) | copy-start | bytes 1540
  30.7 10.0 %collective-permute-start = (bf16[177,1024]{1,0:T(8,128)(2,1)S(1)}, bf16[177,1024]{1,0:T(8,128)(2,1)S(1)}, u32[]{:S(2)}, u32[]{:S(2)}) collective-permute-start(bf16[177,1024]{1,0:T(8,128)(2,1)S(1)} %get-tuple-element.33), channel_id=1, source_target_pairs={{0,4},{4,8},{8,12},{12,16},{16,20},{20,24},{24,28},{1,5},{5,9},{9,... | collective-permute-start | bytes 1087496 | tf_op jit(solution)/shard_map/ppermute | solution.py:30
  36.2 10.2 %collective-permute-start.1 = (bf16[177,1024]{1,0:T(8,128)(2,1)S(1)}, bf16[177,1024]{1,0:T(8,128)(2,1)S(1)}, u32[]{:S(2)}, u32[]{:S(2)}) collective-permute-start(bf16[177,1024]{1,0:T(8,128)(2,1)S(1)} %get-tuple-element.34), channel_id=1, source_target_pairs={{4,0},{8,4},{12,8},{16,12},{20,16},{24,20},{28,24},{5,1},{9,5},{13... | collective-permute-start | bytes 1087496 | tf_op jit(solution)/shard_map/ppermute | solution.py:33
  40.7 31.6 %copy-start.1 = (bf16[177,1024]{1,0:T(8,128)(2,1)}, bf16[177,1024]{1,0:T(8,128)(2,1)S(1)}, u32[]{:S(2)}) copy-start(bf16[177,1024]{1,0:T(8,128)(2,1)S(1)} %collective-permute-done) | copy-start | bytes 1087492
  46.4 26.1 %copy-start.2 = (bf16[177,1024]{1,0:T(8,128)(2,1)}, bf16[177,1024]{1,0:T(8,128)(2,1)S(1)}, u32[]{:S(2)}) copy-start(bf16[177,1024]{1,0:T(8,128)(2,1)S(1)} %collective-permute-done.1) | copy-start | bytes 1087492
  85.1 1.3 %slice-start = ((bf16[177,1024]{1,0:T(8,128)(2,1)}), bf16[80,1024]{1,0:T(8,128)(2,1)S(1)}, s32[]{:S(2)}) async-start(bf16[177,1024]{1,0:T(8,128)(2,1)} %copy-done.1), calls=%async_computation.1 | async-start | bytes 327680 | tf_op jit(solution)/shard_map/slice | solution.py:165
  85.1 1.3 %slice-start.1 = ((bf16[177,1024]{1,0:T(8,128)(2,1)}), bf16[80,1024]{1,0:T(8,128)(2,1)S(1)}, s32[]{:S(2)}) async-start(bf16[177,1024]{1,0:T(8,128)(2,1)} %copy-done.2), calls=%async_computation.2 | async-start | bytes 327680 | tf_op jit(solution)/shard_map/slice | solution.py:166
  99.2 1.7 %copy-start.8 = (bf16[80,80]{1,0:T(8,128)(2,1)S(1)}, bf16[80,80]{1,0:T(8,128)(2,1)}, u32[]{:S(2)}) copy-start(bf16[80,80]{1,0:T(8,128)(2,1)} %param.22) | copy-start | bytes 38404
  99.3 1.7 %copy-start.10 = (f32[96]{0:T(128)S(1)}, f32[96]{0:T(128)}, u32[]{:S(2)}) copy-start(f32[96]{0:T(128)} %param.25) | copy-start | bytes 1156
  99.3 1.7 %copy-start.11 = (f32[80]{0:T(128)S(1)}, f32[80]{0:T(128)}, u32[]{:S(2)}) copy-start(f32[80]{0:T(128)} %param.23) | copy-start | bytes 964
